TPU v7x, 32 devices: a whole 2x2x4 slice. The times are simulated.
32 devices in a mesh: bank: 4 (over y, x), zero: 8 (over z, core).
Axes of the slice: x: 2, y: 2, z: 4, core: 2. Of those that a mesh axis runs over, the one named last changes fastest.
Arguments:
- train_gate: float32 [64, 2048, 1024], P('bank', 'zero'), may hold values from -0.1875 to 0.1875
- train_up: float32 [64, 2048, 1024], P('bank', 'zero'), may hold values from -0.1875 to 0.1875
- train_down: float32 [64, 1024, 2048], P('bank', None, 'zero'), may hold values from -0.25 to 0.25
- router_weight: float32 [2048, 64], P('zero', 'bank'), may hold values from -0.125 to 0.125
- router_gain: float32 [2048], P('zero'), may hold values from 0.25 to 1.75
Outputs:
- ready_gate: bfloat16 [64, 2048, 1024], P('bank', None, 'zero')
- ready_up: bfloat16 [64, 2048, 1024], P('bank', None, 'zero')
- ready_down: bfloat16 [64, 1024, 2048], P('bank', 'zero')
- scale_gate: float32 [64, 1024], P('bank', 'zero')
- scale_up: float32 [64, 1024], P('bank', 'zero')
- scale_down: float32 [64, 1024], P('bank', 'zero')
- serve_router: bfloat16 [2048, 64], replicated
All inputs are finite; a program needn't handle non-finite values.
Results may differ from a plain program's by a relative error of at most 0.001.
Values may be sent and summed in bfloat16 or wider, within the bound.
A program may use at most 192 MiB of HBM per device.

v0:
```python
import jax
import jax.numpy as jnp
from jax import lax
from jax.sharding import PartitionSpec as P


def on_device(train_gate, train_up, train_down, router_weight, router_gain):
    total_gate, total_up, total_down = lax.psum(
        (
            jnp.sum(train_gate * train_gate, axis=1),
            jnp.sum(train_up * train_up, axis=1),
            jnp.sum(train_down * train_down, axis=2),
        ),
        "zero",
    )
    scale_gate = jnp.sqrt(total_gate)
    scale_up = jnp.sqrt(total_up)
    scale_down = jnp.sqrt(total_down)
    narrow_gate, narrow_up, narrow_down = (
        (train_gate / jnp.expand_dims(scale_gate, 1)).astype(jnp.bfloat16),
        (train_up / jnp.expand_dims(scale_up, 1)).astype(jnp.bfloat16),
        (train_down / jnp.expand_dims(scale_down, 2)).astype(jnp.bfloat16),
    )
    ready_gate, ready_up = (
        lax.all_to_all(narrow_gate, "zero", split_axis=2, concat_axis=1, tiled=True),
        lax.all_to_all(narrow_up, "zero", split_axis=2, concat_axis=1, tiled=True),
    )
    ready_down = lax.all_to_all(narrow_down, "zero", split_axis=1, concat_axis=2, tiled=True)
    scale_gate = lax.dynamic_slice_in_dim(
        scale_gate, lax.axis_index("zero") * ready_gate.shape[2], ready_gate.shape[2], axis=1
    )
    scale_up = lax.dynamic_slice_in_dim(
        scale_up, lax.axis_index("zero") * ready_up.shape[2], ready_up.shape[2], axis=1
    )
    scale_down = lax.dynamic_slice_in_dim(
        scale_down, lax.axis_index("zero") * ready_down.shape[1], ready_down.shape[1], axis=1
    )
    part_router = (router_weight * router_gain[:, None]).astype(jnp.bfloat16)
    row_router = lax.all_gather(part_router, "zero", axis=0, tiled=True)
    serve_router = lax.all_gather(row_router, "bank", axis=1, tiled=True)
    return (ready_gate, ready_up, ready_down, scale_gate, scale_up, scale_down, serve_router)


def solution(mesh):
    return jax.shard_map(
        on_device,
        mesh=mesh,
        in_specs=(
            P("bank", "zero", None),
            P("bank", "zero", None),
            P("bank", None, "zero"),
            P("zero", "bank"),
            P("zero"),
        ),
        out_specs=(
            P("bank", None, "zero"),
            P("bank", None, "zero"),
            P("bank", "zero", None),
            P("bank", "zero"),
            P("bank", "zero"),
            P("bank", "zero"),
            P(),
        ),
        check_vma=False,
    )
```

profile of v0, /device:TPU:0, one launch (start us, length us, event | category | flops | bytes accessed | tf_op | source)
XLA Modules:
  0.0 737.8 jit_solution(13230997140834230480)
XLA Ops:
  7.2 8.6 %multiply_reduce_fusion = f32[16,1024]{1,0:T(8,128)} fusion(f32[16,1024,256]{2,1,0:T(8,128)} %param.7), kind=kLoop, calls=%fused_computation.2 | loop fusion | flops 8372224 | bytes 16842752 | tf_op jit(solution)/shard_map/reduce_sum | solution.py:12
  15.8 12.6 %multiply_reduce_fusion.1 = (f32[16,1024]{1,0:T(8,128)}, f32[16,1024]{1,0:T(8,128)}) fusion(f32[16,256,1024]{2,1,0:T(8,128)} %param.6, f32[16,256,1024]{2,1,0:T(8,128)} %param.5), kind=kLoop, calls=%fused_computation.4 | loop fusion | flops 16744448 | bytes 33685504 | tf_op jit(solution)/shard_map/reduce_sum | solution.py:11
  28.4 17.6 %copy.19 = f32[16,256,1024]{1,0,2:T(8,128)} copy(f32[16,256,1024]{2,1,0:T(8,128)} %param.6) | data formatting | bytes 33554432 | tf_op args[1]
  46.1 40.7 %all-reduce.3.cloned.1.call-done = (f32[16,1024]{1,0:T(8,128)}, f32[16,1024]{1,0:T(8,128)}, f32[16,1024]{1,0:T(8,128)}) async-done(((f32[16,1024]{1,0:T(8,128)}, f32[16,1024]{1,0:T(8,128)}, f32[16,1024]{1,0:T(8,128)}), (f32[16,1024]{1,0:T(8,128)}, f32[16,1024]{1,0:T(8,128)}, f32[16,1024]{1,0:T(8,128)})) %all-reduce.3.cloned.1.call-update) | async-done | bytes 196624 | tf_op jit(solution)/shard_map/psum | solution.py:8
  86.8 0.9 sqrt.10
  87.8 9.6 %divide_convert_fusion = bf16[16,256,1024]{1,0,2:T(8,128)(2,1)} fusion(f32[16,256,1024]{1,0,2:T(8,128)} %copy.19, f32[16,1024]{0,1:T(8,128)S(1)} %copy.18), kind=kLoop, calls=%fused_computation.3 | loop fusion | flops 8388608 | bytes 25231360 | tf_op jit(solution)/shard_map/convert_element_type | solution.py:21
  97.5 4.9 all-to-all-start.1
  102.4 17.6 %copy.16 = f32[16,256,1024]{1,0,2:T(8,128)} copy(f32[16,256,1024]{2,1,0:T(8,128)} %param.5) | data formatting | bytes 33554432 | tf_op args[0]
  120.3 9.7 %divide_convert_fusion.1 = bf16[16,256,1024]{1,0,2:T(8,128)(2,1)} fusion(f32[16,256,1024]{1,0,2:T(8,128)} %copy.16, f32[16,1024]{0,1:T(8,128)S(1)} %copy.15), kind=kLoop, calls=%fused_computation.5 | loop fusion | flops 8388608 | bytes 25231360 | tf_op jit(solution)/shard_map/convert_element_type | solution.py:20
  130.0 156.3 %all-to-all-done.1 = bf16[16,256,1024]{1,0,2:T(8,128)(2,1)} async-done(((bf16[16,256,1024]{1,0,2:T(8,128)(2,1)}), bf16[16,256,1024]{1,0,2:T(8,128)(2,1)}, u32[]{:S(2)}, u32[]{:S(2)}) %all-to-all-start.1) | async-done | bytes 8388640 | tf_op jit(solution)/shard_map/all_to_all | solution.py:26
  286.3 4.9 all-to-all-start
  291.5 16.6 %fusion = bf16[16,1024,256]{2,0,1:T(8,128)(2,1)} fusion(f32[16,1024,256]{2,1,0:T(8,128)} %param.7, f32[16,1024]{0,1:T(8,128)S(1)} %copy.21), kind=kLoop, calls=%fused_computation.1 | loop fusion | flops 8388608 | bytes 25231360 | tf_op jit(solution)/shard_map/convert_element_type | solution.py:22
  308.1 167.0 %all-to-all-done = bf16[16,256,1024]{1,0,2:T(8,128)(2,1)} async-done(((bf16[16,256,1024]{1,0,2:T(8,128)(2,1)}), bf16[16,256,1024]{1,0,2:T(8,128)(2,1)}, u32[]{:S(2)}, u32[]{:S(2)}) %all-to-all-start) | async-done | bytes 8388640 | tf_op jit(solution)/shard_map/all_to_all | solution.py:25
  475.1 5.0 all-to-all-start.2
  480.2 189.9 %all_gather.6 = bf16[2048,16]{0,1:T(8,128)(2,1)S(1)} all-gather(bf16[256,16]{0,1:T(8,128)(2,1)S(1)} %multiply_convert_fusion), channel_id=1, replica_groups=mesh['bank'=4,'zero'=8] {'zero'}, dimensions={0}, use_global_device_ids=true | all-gather | bytes 73728 | tf_op jit(solution)/shard_map/all_gather | solution.py:39
  670.0 9.1 %all_gather.7 = bf16[2048,64]{0,1:T(8,128)(2,1)S(1)} all-gather(bf16[2048,16]{0,1:T(8,128)(2,1)S(1)} %all_gather.6), channel_id=1, replica_groups=mesh['bank'=4,'zero'=8] {'bank'}, dimensions={1}, use_global_device_ids=true | all-gather | bytes 327680 | tf_op jit(solution)/shard_map/all_gather | solution.py:40
  679.1 0.6 constant_dynamic-slice_fusion
  679.7 0.6 constant_dynamic-slice_fusion.1
  680.3 0.6 constant_dynamic-slice_fusion.2
  680.9 12.3 %copy.20 = bf16[16,8,256,128]{3,2,1,0:T(8,128)(2,1)} copy(bf16[16,8,256,128]{2,0,3,1:T(8,128)(2,1)} %bitcast.4) | data formatting | bytes 16777216 | tf_op jit(solution)/shard_map/all_to_all | solution.py:26
  693.2 12.3 %copy.17 = bf16[16,8,256,128]{3,2,1,0:T(8,128)(2,1)} copy(bf16[16,8,256,128]{2,0,3,1:T(8,128)(2,1)} %bitcast.1) | data formatting | bytes 16777216 | tf_op jit(solution)/shard_map/all_to_all | solution.py:25
  705.5 11.4 %copy.23 = bf16[16,128,8,256]{3,2,1,0:T(8,128)(2,1)} copy(bf16[16,128,8,256]{3,0,1,2:T(8,128)(2,1)} %bitcast.7) | data formatting | bytes 16777216 | tf_op jit(solution)/shard_map/all_to_all | solution.py:28
  716.9 13.4 %all_to_all.50 = bf16[16,128,2048]{2,1,0:T(8,128)(2,1)} reshape(bf16[16,128,8,256]{3,2,1,0:T(8,128)(2,1)} %copy.23) | data formatting | bytes 16777216 | tf_op jit(solution)/shard_map/all_to_all | solution.py:28
  730.3 0.7 copy.31
  (17 shorter events, 0.7 us)
Async XLA Ops:
  7.2 79.6 %all-reduce.3.cloned.1.call-start = ((), (), s32[]{:S(2)}) async-start(), calls=%async_computation.3 | async-start | bytes 393216 | tf_op jit(solution)/shard_map/psum | solution.py:8
  97.5 188.8 %all-to-all-start.1 = ((bf16[16,256,1024]{1,0,2:T(8,128)(2,1)}), bf16[16,256,1024]{1,0,2:T(8,128)(2,1)}, u32[]{:S(2)}, u32[]{:S(2)}) async-start(bf16[16,256,1024]{1,0,2:T(8,128)(2,1)} %divide_convert_fusion), calls=%async_computation.1 | async-start | bytes 16777216 | tf_op jit(solution)/shard_map/all_to_all | solution.py:26
  102.4 17.6 %copy-start.1 = (f32[16,1024]{1,0:T(8,128)S(1)}, f32[16,1024]{1,0:T(8,128)}, u32[]{:S(2)}) copy-start(f32[16,1024]{1,0:T(8,128)} %get-tuple-element.7) | copy-start | bytes 196612
  120.3 170.9 %copy-start = (f32[16,1024]{1,0:T(8,128)S(1)}, f32[16,1024]{1,0:T(8,128)}, u32[]{:S(2)}) copy-start(f32[16,1024]{1,0:T(8,128)} %get-tuple-element.9) | copy-start | bytes 196612
  286.3 188.8 %all-to-all-start = ((bf16[16,256,1024]{1,0,2:T(8,128)(2,1)}), bf16[16,256,1024]{1,0,2:T(8,128)(2,1)}, u32[]{:S(2)}, u32[]{:S(2)}) async-start(bf16[16,256,1024]{1,0,2:T(8,128)(2,1)} %divide_convert_fusion.1), calls=%async_computation | async-start | bytes 16777216 | tf_op jit(solution)/shard_map/all_to_all | solution.py:25
  291.5 188.6 %copy-start.2 = (f32[256,16]{0,1:T(8,128)S(1)}, f32[256,16]{0,1:T(8,128)}, u32[]{:S(2)}) copy-start(f32[256,16]{0,1:T(8,128)} %param.8) | copy-start | bytes 49156
  291.5 188.6 %copy-start.3 = (f32[256]{0:T(256)S(1)}, f32[256]{0:T(256)}, u32[]{:S(2)}) copy-start(f32[256]{0:T(256)} %param.9) | copy-start | bytes 3076
  475.1 230.4 %all-to-all-start.2 = ((bf16[16,1024,256]{2,0,1:T(8,128)(2,1)}), bf16[16,1024,256]{2,0,1:T(8,128)(2,1)}, u32[]{:S(2)}, u32[]{:S(2)}) async-start(bf16[16,1024,256]{2,0,1:T(8,128)(2,1)} %fusion), calls=%async_computation.2 | async-start | bytes 16777216 | tf_op jit(solution)/shard_map/all_to_all | solution.py:28
Sparse Core Ops, SparseCore 0:
  28.6 58.1 all-reduce.2
where the time goes:
time: 740 us; the launch traced here: 738 us
  waiting for transfers between devices  364 us (49%)
  blocking collectives  199 us (27%)
  local copies, waits for them, and re-layouts  88.6 us (12%)
  other arithmetic  57.2 us (8%)
  starting transfers between devices  14.9 us (2%)
  between operations  14.2 us (2%)
    all_gather x1, blocking collectives, on_device(): row_router = lax.all_gather(part_router, 'zero', axis=0, tiled=True)  190 us
    all_to_all x1, waiting for transfers between devices, on_device(): lax.all_to_all(narrow_gate, 'zero', split_axis=2, concat_axis=1, tiled=True)  167 us
    all_to_all x1, waiting for transfers between devices, on_device(): lax.all_to_all(narrow_up, 'zero', split_axis=2, concat_axis=1, tiled=True)  156 us
    psum x1, waiting for transfers between devices, on_device(): lax.psum((jnp.sum(train_gate * train_gate, axis=1), jnp.sum(train_up * tr...  40.7 us
    unnamed x11, local copies, waits for them, and re-layouts  36 us
    all_to_all x2, local copies, waits for them, and re-layouts, on_device(): lax.all_to_all(narrow_down, 'zero', split_axis=1, concat_axis=2, tiled=True)  24.8 us
    convert_element_type x1, other arithmetic, on_device(): (train_down / jnp.expand_dims(scale_down, 2)).astype(jnp.bfloat16)  16.6 us
  transfers between devices with their start and end apart: 4, of which 3 were waited for; matrix products, arithmetic and copies ran while one was open for 12% of the time, Pallas kernels for 0%

commit v1 on v0

--- a/solution.py
+++ b/solution.py
@@ -37,7 +37,9 @@
     )
     part_router = (router_weight * router_gain[:, None]).astype(jnp.bfloat16)
     row_router = lax.all_gather(part_router, "zero", axis=0, tiled=True)
-    serve_router = lax.all_gather(row_router, "bank", axis=1, tiled=True)
+    serve_router = jnp.concatenate(
+        lax.all_to_all(jnp.stack(lax.axis_size("bank") * [row_router]), "bank", 0, 0), axis=1
+    )
     return (ready_gate, ready_up, ready_down, scale_gate, scale_up, scale_down, serve_router)
 
 

time: 740 us -> 698 us (0.943)
  blocking collectives: 199 us -> 15.7 us
  waiting for transfers between devices: 364 us -> 501 us
    all_gather x1, blocking collectives: 190 us -> 15.7 us  [on_device(): row_router = lax.all_gather(part_router, 'zero', axis=0, tiled=True)]
    all_to_all x1, waiting for transfers between devices: 0.01 us -> 157 us  [on_device(): lax.all_to_all(narrow_down, 'zero', split_axis=1, concat_axis=2, tiled=True)]
    psum x1, waiting for transfers between devices: 40.7 us -> 20.6 us  [on_device(): lax.psum((jnp.sum(train_gate * train_gate, axis=1), jnp.sum(train_up * tr...]
    all_gather x1 -> x0, blocking collectives: 9.11 us -> none  [on_device(): serve_router = lax.all_gather(row_router, 'bank', axis=1, tiled=True)]
  transfers between devices with their start and end apart: 4 -> 5, of which waited for: 3 -> 4; matrix products, arithmetic and copies ran while one was open for 12% -> 14% of each run, Pallas kernels for 0% -> 0%
where the time goes in v1:
time: 698 us; the launch traced here: 696 us
  waiting for transfers between devices  501 us (72%)
  local copies, waits for them, and re-layouts  89.3 us (13%)
  other arithmetic  57.2 us (8%)
  starting transfers between devices  18.9 us (3%)
  blocking collectives  15.7 us (2%)
  between operations  14.2 us (2%)
    all_to_all x1, waiting for transfers between devices, on_device(): lax.all_to_all(narrow_gate, 'zero', split_axis=2, concat_axis=1, tiled=True)  167 us
    all_to_all x1, waiting for transfers between devices, on_device(): lax.all_to_all(narrow_down, 'zero', split_axis=1, concat_axis=2, tiled=True)  157 us
    all_to_all x1, waiting for transfers between devices, on_device(): lax.all_to_all(narrow_up, 'zero', split_axis=2, concat_axis=1, tiled=True)  156 us
    unnamed x11, local copies, waits for them, and re-layouts  35.9 us
    all_to_all x2, local copies, waits for them, and re-layouts, on_device(): lax.all_to_all(narrow_down, 'zero', split_axis=1, concat_axis=2, tiled=True)  24.8 us
    psum x1, waiting for transfers between devices, on_device(): lax.psum((jnp.sum(train_gate * train_gate, axis=1), jnp.sum(train_up * tr...  20.6 us
    convert_element_type x1, other arithmetic, on_device(): (train_down / jnp.expand_dims(scale_down, 2)).astype(jnp.bfloat16)  16.6 us
    all_gather x1, blocking collectives, on_device(): row_router = lax.all_gather(part_router, 'zero', axis=0, tiled=True)  15.7 us
  transfers between devices with their start and end apart: 5, of which 4 were waited for; matrix products, arithmetic and copies ran while one was open for 14% of the time, Pallas kernels for 0%

profile of v1, /device:TPU:0, one launch (start us, length us, event | category | flops | bytes accessed | tf_op | source)
XLA Modules:
  0.0 696.4 jit_solution(11741633743572028333)
XLA Ops:
  7.2 8.6 %multiply_reduce_fusion = f32[16,1024]{1,0:T(8,128)} fusion(f32[16,1024,256]{2,1,0:T(8,128)} %param.7), kind=kLoop, calls=%fused_computation.2 | loop fusion | flops 8372224 | bytes 16842752 | tf_op jit(solution)/shard_map/reduce_sum | solution.py:12
  15.9 12.6 %multiply_reduce_fusion.1 = (f32[16,1024]{1,0:T(8,128)}, f32[16,1024]{1,0:T(8,128)}) fusion(f32[16,256,1024]{2,1,0:T(8,128)} %param.6, f32[16,256,1024]{2,1,0:T(8,128)} %param.5), kind=kLoop, calls=%fused_computation.4 | loop fusion | flops 16744448 | bytes 33685504 | tf_op jit(solution)/shard_map/reduce_sum | solution.py:11
  28.5 15.7 %all_gather.3 = bf16[2048,16]{0,1:T(8,128)(2,1)S(1)} all-gather(bf16[256,16]{0,1:T(8,128)(2,1)S(1)} %multiply_convert_fusion), channel_id=1, replica_groups=mesh['bank'=4,'zero'=8] {'zero'}, dimensions={0}, use_global_device_ids=true | all-gather | bytes 73728 | tf_op jit(solution)/shard_map/all_gather | solution.py:39
  44.2 0.7 stack.2
  44.9 3.7 all-to-all-start.3
  48.6 17.6 %copy.19 = f32[16,256,1024]{1,0,2:T(8,128)} copy(f32[16,256,1024]{2,1,0:T(8,128)} %param.6) | data formatting | bytes 33554432 | tf_op args[1]
  66.2 20.6 %all-reduce.3.cloned.1.call-done = (f32[16,1024]{1,0:T(8,128)}, f32[16,1024]{1,0:T(8,128)}, f32[16,1024]{1,0:T(8,128)}) async-done(((f32[16,1024]{1,0:T(8,128)}, f32[16,1024]{1,0:T(8,128)}, f32[16,1024]{1,0:T(8,128)}), (f32[16,1024]{1,0:T(8,128)}, f32[16,1024]{1,0:T(8,128)}, f32[16,1024]{1,0:T(8,128)})) %all-reduce.3.cloned.1.call-update) | async-done | bytes 196624 | tf_op jit(solution)/shard_map/psum | solution.py:8
  86.8 0.9 sqrt.10
  87.8 9.6 %divide_convert_fusion = bf16[16,256,1024]{1,0,2:T(8,128)(2,1)} fusion(f32[16,256,1024]{1,0,2:T(8,128)} %copy.19, f32[16,1024]{0,1:T(8,128)S(1)} %copy.18), kind=kLoop, calls=%fused_computation.3 | loop fusion | flops 8388608 | bytes 25231360 | tf_op jit(solution)/shard_map/convert_element_type | solution.py:21
  97.5 5.0 all-to-all-start.1
  102.5 17.6 %copy.16 = f32[16,256,1024]{1,0,2:T(8,128)} copy(f32[16,256,1024]{2,1,0:T(8,128)} %param.5) | data formatting | bytes 33554432 | tf_op args[0]
  120.3 9.7 %divide_convert_fusion.1 = bf16[16,256,1024]{1,0,2:T(8,128)(2,1)} fusion(f32[16,256,1024]{1,0,2:T(8,128)} %copy.16, f32[16,1024]{0,1:T(8,128)S(1)} %copy.15), kind=kLoop, calls=%fused_computation.5 | loop fusion | flops 8388608 | bytes 25231360 | tf_op jit(solution)/shard_map/convert_element_type | solution.py:20
  130.0 156.3 %all-to-all-done.1 = bf16[16,256,1024]{1,0,2:T(8,128)(2,1)} async-done(((bf16[16,256,1024]{1,0,2:T(8,128)(2,1)}), bf16[16,256,1024]{1,0,2:T(8,128)(2,1)}, u32[]{:S(2)}, u32[]{:S(2)}) %all-to-all-start.1) | async-done | bytes 8388640 | tf_op jit(solution)/shard_map/all_to_all | solution.py:26
  286.3 4.9 all-to-all-start
  291.5 16.6 %fusion = bf16[16,1024,256]{2,0,1:T(8,128)(2,1)} fusion(f32[16,1024,256]{2,1,0:T(8,128)} %param.7, f32[16,1024]{0,1:T(8,128)S(1)} %copy.21), kind=kLoop, calls=%fused_computation.1 | loop fusion | flops 8388608 | bytes 25231360 | tf_op jit(solution)/shard_map/convert_element_type | solution.py:22
  308.1 167.0 %all-to-all-done = bf16[16,256,1024]{1,0,2:T(8,128)(2,1)} async-done(((bf16[16,256,1024]{1,0,2:T(8,128)(2,1)}), bf16[16,256,1024]{1,0,2:T(8,128)(2,1)}, u32[]{:S(2)}, u32[]{:S(2)}) %all-to-all-start) | async-done | bytes 8388640 | tf_op jit(solution)/shard_map/all_to_all | solution.py:25
  475.1 5.2 all-to-all-start.2
  480.3 0.6 constant_dynamic-slice_fusion
  482.2 12.3 %copy.20 = bf16[16,8,256,128]{3,2,1,0:T(8,128)(2,1)} copy(bf16[16,8,256,128]{2,0,3,1:T(8,128)(2,1)} %bitcast.4) | data formatting | bytes 16777216 | tf_op jit(solution)/shard_map/all_to_all | solution.py:26
  494.4 12.3 %copy.17 = bf16[16,8,256,128]{3,2,1,0:T(8,128)(2,1)} copy(bf16[16,8,256,128]{2,0,3,1:T(8,128)(2,1)} %bitcast.1) | data formatting | bytes 16777216 | tf_op jit(solution)/shard_map/all_to_all | solution.py:25
  506.7 157.3 %all-to-all-done.2 = bf16[16,1024,256]{2,0,1:T(8,128)(2,1)} async-done(((bf16[16,1024,256]{2,0,1:T(8,128)(2,1)}), bf16[16,1024,256]{2,0,1:T(8,128)(2,1)}, u32[]{:S(2)}, u32[]{:S(2)}) %all-to-all-start.2) | async-done | bytes 8388640 | tf_op jit(solution)/shard_map/all_to_all | solution.py:28
  664.0 11.4 %copy.23 = bf16[16,128,8,256]{3,2,1,0:T(8,128)(2,1)} copy(bf16[16,128,8,256]{3,0,1,2:T(8,128)(2,1)} %bitcast.7) | data formatting | bytes 16777216 | tf_op jit(solution)/shard_map/all_to_all | solution.py:28
  675.4 13.4 %all_to_all.53 = bf16[16,128,2048]{2,1,0:T(8,128)(2,1)} reshape(bf16[16,128,8,256]{3,2,1,0:T(8,128)(2,1)} %copy.23) | data formatting | bytes 16777216 | tf_op jit(solution)/shard_map/all_to_all | solution.py:28
  688.8 0.7 copy.31
  (19 shorter events, 1.9 us)
Async XLA Ops:
  7.2 79.6 %all-reduce.3.cloned.1.call-start = ((), (), s32[]{:S(2)}) async-start(), calls=%async_computation.4 | async-start | bytes 393216 | tf_op jit(solution)/shard_map/psum | solution.py:8
  15.8 12.6 %copy-start.2 = (f32[256,16]{0,1:T(8,128)S(1)}, f32[256,16]{0,1:T(8,128)}, u32[]{:S(2)}) copy-start(f32[256,16]{0,1:T(8,128)} %param.8) | copy-start | bytes 49156
  15.8 12.6 %copy-start.3 = (f32[256]{0:T(256)S(1)}, f32[256]{0:T(256)}, u32[]{:S(2)}) copy-start(f32[256]{0:T(256)} %param.9) | copy-start | bytes 3076
  44.9 52.6 %all-to-all-start.3 = ((bf16[4,2048,16]{1,2,0:T(8,128)(2,1)}), bf16[4,2048,16]{1,2,0:T(8,128)(2,1)S(1)}, u32[]{:S(2)}, u32[]{:S(2)}) async-start(bf16[4,2048,16]{1,2,0:T(8,128)(2,1)} %stack.2), calls=%async_computation.3 | async-start | bytes 524288 | tf_op jit(solution)/shard_map/all_to_all | solution.py:41
  97.5 188.8 %all-to-all-start.1 = ((bf16[16,256,1024]{1,0,2:T(8,128)(2,1)}), bf16[16,256,1024]{1,0,2:T(8,128)(2,1)}, u32[]{:S(2)}, u32[]{:S(2)}) async-start(bf16[16,256,1024]{1,0,2:T(8,128)(2,1)} %divide_convert_fusion), calls=%async_computation.1 | async-start | bytes 16777216 | tf_op jit(solution)/shard_map/all_to_all | solution.py:26
  102.5 17.6 %copy-start.1 = (f32[16,1024]{1,0:T(8,128)S(1)}, f32[16,1024]{1,0:T(8,128)}, u32[]{:S(2)}) copy-start(f32[16,1024]{1,0:T(8,128)} %get-tuple-element.7) | copy-start | bytes 196612
  120.3 171.0 %copy-start = (f32[16,1024]{1,0:T(8,128)S(1)}, f32[16,1024]{1,0:T(8,128)}, u32[]{:S(2)}) copy-start(f32[16,1024]{1,0:T(8,128)} %get-tuple-element.9) | copy-start | bytes 196612
  286.3 188.8 %all-to-all-start = ((bf16[16,256,1024]{1,0,2:T(8,128)(2,1)}), bf16[16,256,1024]{1,0,2:T(8,128)(2,1)}, u32[]{:S(2)}, u32[]{:S(2)}) async-start(bf16[16,256,1024]{1,0,2:T(8,128)(2,1)} %divide_convert_fusion.1), calls=%async_computation | async-start | bytes 16777216 | tf_op jit(solution)/shard_map/all_to_all | solution.py:25
  475.1 188.9 %all-to-all-start.2 = ((bf16[16,1024,256]{2,0,1:T(8,128)(2,1)}), bf16[16,1024,256]{2,0,1:T(8,128)(2,1)}, u32[]{:S(2)}, u32[]{:S(2)}) async-start(bf16[16,1024,256]{2,0,1:T(8,128)(2,1)} %fusion), calls=%async_computation.2 | async-start | bytes 16777216 | tf_op jit(solution)/shard_map/all_to_all | solution.py:28
Sparse Core Ops, SparseCore 0:
  28.6 58.1 all-reduce.2
